TPU v7x, 32 devices: a whole 2x2x4 slice. The times are simulated.
32 devices in a mesh: row: 4 (over y, core), col: 8 (over z, x).
Axes of the slice: x: 2, y: 2, z: 4, core: 2. Of those that a mesh axis runs over, the one named last changes fastest.
Arguments:
- velocity_modes: bfloat16 [3, 176, 352, 704], P(None, 'row', 'col'), may hold values from -0.00090789795 to 0.00090789795
- wavenumbers: float32 [8], replicated, may hold values from 0.5 to 3
- polar: float32 [8], replicated, may hold values from -3.140625 to 3.140625
- azimuth: float32 [8], replicated, may hold values from -3.140625 to 3.140625
Outputs:
- velocity: bfloat16 [3, 512, 512, 512], P(None, 'row', 'col')
- far_field: float32 [8, 2, 8], P('col')
All inputs are finite; a program needn't handle non-finite values.
Results may differ from a plain program's by a relative error of at most 0.0075.
Values may be sent and summed in bfloat16 or wider, within the bound.
A program may use at most 192 MiB of HBM per device.

v0:
```python
import math

import jax
import jax.numpy as jnp
from jax import lax
from jax.sharding import PartitionSpec as P

N = 512
M = 352
KX = 176
FREQS = 8


def complex_table(modes, points):
    waves = jnp.arange(modes, dtype=jnp.int32) - modes // 2
    cells = jnp.arange(points, dtype=jnp.int32)
    product = jnp.mod(waves[:, None] * cells[None, :], points)
    angle = product.astype(jnp.float32) * (2.0 * math.pi / points)
    cosine = jnp.cos(angle)
    sine = jnp.sin(angle)
    table = jnp.stack([jnp.stack([cosine, sine], 1), jnp.stack([-sine, cosine], 1)], 0)
    return table.astype(jnp.bfloat16)


def half_table(count, points):
    waves = jnp.arange(count, dtype=jnp.int32)
    cells = jnp.arange(points, dtype=jnp.int32)
    product = jnp.mod(waves[:, None] * cells[None, :], points)
    angle = product.astype(jnp.float32) * (2.0 * math.pi / points)
    cosine = jnp.cos(angle).astype(jnp.bfloat16)
    sine = jnp.sin(angle).astype(jnp.bfloat16)
    factor = jnp.where(waves == 0, 1.0, 2.0).astype(jnp.bfloat16)[:, None]
    return jnp.stack([factor * cosine, -(factor * sine)], 0)


def stresses(field):
    trace = (field[0] * field[0] + field[1] * field[1] + field[2] * field[2]) / 3.0
    parts = [
        field[0] * field[0] - trace,
        field[1] * field[1] - trace,
        field[2] * field[2] - trace,
        field[0] * field[1],
        field[0] * field[2],
        field[1] * field[2],
    ]
    return jnp.stack(parts, 0).astype(jnp.bfloat16)


def far_terms(stress, wave_j, axis_one, axis_two, axis_three, y_pos, z_pos):
    points = stress.shape[-1]
    y_count = stress.shape[1]
    z_count = stress.shape[2]
    count = wave_j.shape[0]
    x_pos = jnp.arange(points, dtype=jnp.int32).astype(jnp.float32) * (2.0 * math.pi / points)
    angle_x = wave_j[None, :] * (axis_one[None, :] * x_pos[:, None])
    phase_x = (
        jnp.stack([jnp.cos(angle_x), -jnp.sin(angle_x)], 1)
        .reshape(points, 2 * count)
        .astype(jnp.bfloat16)
    )
    lines = jnp.dot(
        stress.reshape(6 * y_count * z_count, points), phase_x, preferred_element_type=jnp.float32
    )
    lines = lines.reshape(6, y_count, z_count, 2, count)
    weights = [
        axis_one * axis_one,
        axis_two * axis_two,
        axis_three * axis_three,
        2.0 * axis_one * axis_two,
        2.0 * axis_one * axis_three,
        2.0 * axis_two * axis_three,
    ]
    mixed = weights[0][None, None, None, :] * lines[0]
    for index in range(1, 6):
        mixed = mixed + weights[index][None, None, None, :] * lines[index]
    angle = wave_j[None, None, :] * (axis_two[None, None, :] * y_pos[:, None, None]) + wave_j[
        None, None, :
    ] * (axis_three[None, None, :] * z_pos[None, :, None])
    cosine = jnp.cos(angle)
    sine = jnp.sin(angle)
    real_part = mixed[:, :, 0, :]
    imag_part = mixed[:, :, 1, :]
    return jnp.stack(
        [
            jnp.sum(real_part * cosine + imag_part * sine, (0, 1)),
            jnp.sum(imag_part * cosine - real_part * sine, (0, 1)),
        ],
        0,
    )


def body(velocity_modes, wavenumbers, polar, azimuth):
    table = complex_table(M, N)
    table_x = half_table(KX, N)
    rows_kx = velocity_modes.shape[1]
    cols_ky = velocity_modes.shape[2]
    modes = velocity_modes.reshape(3, rows_kx, cols_ky, 2, M)
    first = jnp.einsum(
        "cabpk,pkqz->caqbz", modes, table, preferred_element_type=jnp.float32
    ).astype(jnp.bfloat16)
    moved = lax.all_to_all(first, "col", split_axis=4, concat_axis=3, tiled=True)
    second = jnp.einsum(
        "caqbz,qbpy->cazpy", moved, table, preferred_element_type=jnp.float32
    ).astype(jnp.bfloat16)
    arrived = lax.all_to_all(second, "row", split_axis=4, concat_axis=1, tiled=True)
    field = jnp.einsum("cazpy,pax->cyzx", arrived, table_x, preferred_element_type=jnp.float32)
    velocity = field.astype(jnp.bfloat16)
    stress = stresses(field)
    y_local = field.shape[1]
    z_local = field.shape[2]
    dirs = polar.shape[0]
    wave_j = jnp.repeat(wavenumbers, dirs)
    axis_one = jnp.tile(jnp.sin(polar) * jnp.cos(azimuth), FREQS)
    axis_two = jnp.tile(jnp.sin(polar) * jnp.sin(azimuth), FREQS)
    axis_three = jnp.tile(jnp.cos(polar), FREQS)
    y_index = lax.axis_index("row") * y_local + jnp.arange(y_local, dtype=jnp.int32)
    z_index = lax.axis_index("col") * z_local + jnp.arange(z_local, dtype=jnp.int32)
    y_pos = y_index.astype(jnp.float32) * (2.0 * math.pi / N)
    z_pos = z_index.astype(jnp.float32) * (2.0 * math.pi / N)
    terms = far_terms(stress, wave_j, axis_one, axis_two, axis_three, y_pos, z_pos)
    spectrum = terms.reshape(2, FREQS, dirs) * (wavenumbers * wavenumbers)[None, :, None] / N**1.5
    partial_sum = jnp.transpose(spectrum, (2, 0, 1))
    owned = lax.psum_scatter(partial_sum, "col", scatter_dimension=0, tiled=True)
    far_field = lax.psum(owned, "row")
    return (velocity, far_field)


def solution(mesh):
    return jax.shard_map(
        body,
        mesh=mesh,
        in_specs=(P(None, "row", "col", None), P(), P(), P()),
        out_specs=(P(None, "row", "col", None), P("col", None, None)),
        check_vma=False,
    )
```

profile of v0, /device:TPU:0, one launch (start us, length us, event | category | flops | bytes accessed | tf_op | source)
XLA Modules:
  0.0 1565.9 jit_solution(17726658873091997270)
XLA Ops:
  0.6 20.4 %reshape.626 = bf16[3,44,44,2,352]{4,3,2,1,0:T(2,128)(2,1)} reshape(bf16[3,44,44,704]{3,2,1,0:T(8,128)(2,1)} %param.4) | data formatting | bytes 16355328 | tf_op jit(solution)/shard_map/reshape | solution.py:97
  21.0 3.3 fusion.38
  24.4 17.3 %fusion.7 = bf16[3,44,2,44,512]{4,3,1,0,2:T(8,128)(2,1)} fusion(bf16[3,44,44,2,352]{4,3,2,1,0:T(2,128)(2,1)} %reshape.626, bf16[1,352,2,512]{3,1,0,2:T(8,128)(2,1)S(1)} %get-tuple-element.23, bf16[1,352,2,512]{3,1,0,2:T(8,128)(2,1)S(1)} %get-tuple-element.22), kind=kOutput, calls=%fused_computation.16 | convolution fusion | flops 8382758912 | bytes 21514240 | tf_op jit(solution)/shard_map/cabpk,pkqz->caqbz/dot_general | solution.py:98
  41.7 70.2 %copy.64 = bf16[3,44,2,44,512]{3,2,1,0,4:T(2,128)(2,1)} copy(bf16[3,44,2,44,512]{4,3,1,0,2:T(8,128)(2,1)} %fusion.7) | data formatting | bytes 23789568 | tf_op jit(solution)/shard_map/convert_element_type | solution.py:100
  111.9 118.5 %reshape.636 = bf16[8,2,371712]{2,1,0:T(2,128)(2,1)} reshape(bf16[512,3,44,2,44]{4,3,2,1,0:T(2,128)(2,1)} %bitcast.97) | data formatting | bytes 23789568
  230.3 267.3 %all_to_all.36 = bf16[8,2,371712]{2,1,0:T(2,128)(2,1)} all-to-all(bf16[8,2,371712]{2,1,0:T(2,128)(2,1)} %reshape.636), channel_id=1, replica_groups=mesh['row'=4,'col'=8] {'col'}, dimensions={0} | all-to-all | bytes 23789568 | tf_op jit(solution)/shard_map/all_to_all | solution.py:101
  497.6 126.0 %reshape.637 = bf16[512,3,44,2,44]{4,3,2,1,0:T(2,128)(2,1)} reshape(bf16[8,2,371712]{2,1,0:T(2,128)(2,1)} %all_to_all.36) | data formatting | bytes 23789568
  623.6 23.6 %copy.101 = bf16[3,44,2,44,8,64]{3,4,5,2,1,0:T(8,128)(2,1)} copy(bf16[3,44,2,44,8,64]{3,2,1,0,5,4:T(2,128)(2,1)} %bitcast.98) | data formatting | bytes 23789568 | tf_op jit(solution)/shard_map/all_to_all | solution.py:101
  647.2 44.0 %reshape.630 = bf16[3,44,2,352,64,1]{3,4,2,1,0,5:T(8,128)(2,1)} reshape(bf16[3,44,2,8,44,64]{4,3,5,2,1,0:T(8,128)(2,1)} %bitcast.99) | data formatting | bytes 23789568 | tf_op jit(solution)/shard_map/all_to_all | solution.py:101
  691.2 21.6 %bitcast_convert_fusion = bf16[3,44,64,2,512]{4,2,3,1,0:T(8,128)(2,1)} fusion(bf16[3,44,2,352,64,1]{3,4,2,1,0,5:T(8,128)(2,1)} %reshape.630, bf16[1,352,2,512]{3,1,0,2:T(8,128)(2,1)S(1)} %get-tuple-element.23, bf16[1,352,2,512]{3,1,0,2:T(8,128)(2,1)S(1)} %get-tuple-element.22), kind=kOutput, calls=%fused_computation | convolution fusion | flops 12191793152 | bytes 30638080 | tf_op jit(solution)/shard_map/caqbz,qbpy->cazpy/dot_general | solution.py:102
  712.9 69.9 %copy.67 = bf16[3,44,64,2,512]{2,3,1,0,4:T(2,128)(2,1)} copy(bf16[3,44,64,2,512]{4,2,3,1,0:T(8,128)(2,1)} %bitcast_convert_fusion) | data formatting | bytes 34603008 | tf_op jit(solution)/shard_map/convert_element_type | solution.py:104
  782.7 48.9 %reshape.638 = bf16[4,2,1081344]{2,1,0:T(2,128)(2,1)} reshape(bf16[512,3,44,2,64]{4,3,2,1,0:T(2,128)(2,1)} %bitcast.95) | data formatting | bytes 34603008
  831.7 7.5 all-to-all-start.1
  841.5 0.7 pad_maximum_fusion.3
  842.8 0.7 multiply_multiply_fusion.1
  843.5 0.7 multiply_multiply_fusion.2
  844.2 1.5 fusion.42
  845.7 182.1 %all-to-all-done.1 = bf16[4,2,1081344]{2,1,0:T(2,128)(2,1)} async-done(((bf16[4,2,1081344]{2,1,0:T(2,128)(2,1)}), bf16[4,2,1081344]{2,1,0:T(2,128)(2,1)}, u32[]{:S(2)}, u32[]{:S(2)}) %all-to-all-start.1) | async-done | bytes 17301536 | tf_op jit(solution)/shard_map/all_to_all | solution.py:105
  1027.8 47.9 %reshape.639 = bf16[512,3,44,2,64]{4,3,2,1,0:T(2,128)(2,1)} reshape(bf16[4,2,1081344]{2,1,0:T(2,128)(2,1)} %all-to-all-done.1) | data formatting | bytes 34603008
  1075.7 83.6 %copy.89 = bf16[3,44,64,2,4,128]{5,4,2,3,1,0:T(4,128)(2,1)} copy(bf16[3,44,64,2,4,128]{2,3,1,0,5,4:T(2,128)(2,1)} %bitcast.96) | data formatting | bytes 34603008 | tf_op jit(solution)/shard_map/all_to_all | solution.py:105
  1159.3 15.6 copy.69
  1174.8 33.4 %fusion.53 = (bf16[3,128,64,512]{3,1,2,0:T(8,128)(2,1)}, f32[3,128,64,512]{3,1,2,0:T(8,128)}) fusion(bf16[3,176,64,2,128]{4,2,3,1,0:T(8,128)(2,1)} %bitcast.100, bf16[1,176,512]{2,1,0:T(8,128)(2,1)S(1)} %get-tuple-element.42, bf16[1,176,512]{2,1,0:T(8,128)(2,1)S(1)} %get-tuple-element.41), kind=kOutput, calls=%fused_computation.97 | convolution fusion | flops 8871673856 | bytes 93159424 | tf_op jit(solution)/shard_map/cazpy,pax->cyzx/dot_general | solution.py:106
  1208.3 26.8 %copy.79 = bf16[3,128,64,512]{3,2,1,0:T(8,128)(2,1)} copy(bf16[3,128,64,512]{3,1,2,0:T(8,128)(2,1)} %get-tuple-element.43) | data formatting | bytes 50331648
  1235.1 20.9 %fusion.10 = (bf16[6,128,64,512]{3,1,2,0:T(8,128)(2,1)}, f32[1,128,64,512]{3,1,2,0:T(8,128)S(1)}) fusion(f32[3,128,64,512]{3,1,2,0:T(8,128)} %get-tuple-element.44), kind=kLoop, calls=%fused_computation.17 | loop fusion | flops 33554432 | bytes 75497472
  1255.9 10.9 fusion.11
  1266.9 11.0 fusion.12
  1277.8 15.0 fusion.13
  1292.9 15.1 fusion.14
  1308.0 15.1 fusion.15
  1323.0 45.4 %copy.71 = bf16[6,128,64,512]{3,2,1,0:T(8,128)(2,1)} copy(bf16[6,128,64,512]{3,1,2,0:T(8,128)(2,1)} %fusion.15) | data formatting | bytes 100663296 | tf_op jit(solution)/shard_map/stack | solution.py:46
  1368.5 30.4 %fusion.54 = f32[49152,128]{1,0:T(8,128)} fusion(bf16[49152,512]{1,0:T(8,128)(2,1)} %bitcast.94, bf16[512,128]{0,1:T(8,128)(2,1)S(1)} %bitcast.102), kind=kOutput, calls=%fused_computation.98 | convolution fusion | flops 6442450944 | bytes 75628544 | tf_op jit(solution)/shard_map/dot_general | solution.py:61
  1398.8 17.2 %fusion.51 = (f32[8192,128]{1,0:T(8,128)}, f32[8192,128]{1,0:T(8,128)}, f32[8192,128]{1,0:T(8,128)}, f32[8192,128]{1,0:T(8,128)}, f32[8192,128]{1,0:T(8,128)}, /*index=5*/f32[8192,128]{1,0:T(8,128)}) fusion(f32[49152,128]{1,0:T(8,128)} %fusion.54), kind=kLoop, calls=%fused_computation.95 | loop fusion | bytes 50331648 | tf_op jit(solution)/shard_map/slice | solution.py:73
  1416.0 5.6 copy.77
  1421.6 7.9 squeeze.21
  1429.5 5.6 copy.76
  1435.1 7.8 squeeze.20
  1442.9 5.6 copy.75
  1448.5 7.9 squeeze.19
  1456.4 5.6 copy.74
  1462.0 7.8 squeeze.18
  1469.8 5.6 copy.73
  1475.5 7.9 squeeze.17
  1483.3 5.8 copy.72
  1489.1 7.8 squeeze.16
  1497.0 22.6 %multiply_add_fusion = f32[128,64,2,64]{1,0,3,2:T(8,128)} fusion(f32[128,64,2,64]{1,0,3,2:T(8,128)} %squeeze.21, f32[128,64,2,64]{1,0,3,2:T(8,128)} %squeeze.20, f32[128,64,2,64]{1,0,3,2:T(8,128)} %squeeze.19, f32[128,64,2,64]{1,0,3,2:T(8,128)} %squeeze.18, f32[128,64,2,64]{1,0,3,2:T(8,128)} %squeeze.17, f32[128,64,2,64]{1,0,3,2:T(8,128)} %squeeze.16, ...), kind=kLoop, calls=%fused_computation.23 | loop fusion | flops 11534336 | bytes 29361664 | tf_op jit(solution)/shard_map/add | solution.py:75
  1519.7 19.8 %fusion.21 = (f32[64]{0:T(128)S(1)}, f32[64]{0:T(128)S(1)}) fusion(f32[128,64,2,64]{1,0,3,2:T(8,128)} %multiply_add_fusion, f32[64,64]{0,1:T(8,128)S(1)} %copy-done.1, f32[128,64]{0,1:T(8,128)S(1)} %copy-done.2), kind=kLoop, calls=%fused_computation.31 | loop fusion | flops 4718464 | bytes 4243968 | tf_op jit(solution)/shard_map/reduce_sum | solution.py:85
  1539.8 19.0 %all-reduce = f32[8,2,8]{2,1,0:T(2,128)S(1)} all-reduce(f32[8,2,8]{2,1,0:T(2,128)S(1)} %copy.78), channel_id=2, replica_groups=mesh['row'=4,'col'=8] {'col'}, use_global_device_ids=true, to_apply=%region_2.3.clone | all-reduce | flops 128 | bytes 1024
  1559.4 6.3 psum.7
  (53 shorter events, 4.0 us)
Async XLA Ops:
  831.7 7.5 copy-start.12
  831.7 7.6 copy-start.11
  831.7 7.7 copy-start.9
  831.7 8.6 copy-start.13
  831.7 196.1 %all-to-all-start.1 = ((bf16[4,2,1081344]{2,1,0:T(2,128)(2,1)}), bf16[4,2,1081344]{2,1,0:T(2,128)(2,1)}, u32[]{:S(2)}, u32[]{:S(2)}) async-start(bf16[4,2,1081344]{2,1,0:T(2,128)(2,1)} %reshape.638), calls=%async_computation.1 | async-start | bytes 34603008 | tf_op jit(solution)/shard_map/all_to_all | solution.py:105
  1323.0 45.4 %copy-start = (bf16[512,2,64]{0,2,1:T(8,128)(2,1)S(1)}, bf16[512,2,64]{0,2,1:T(8,128)(2,1)}, u32[]{:S(2)}) copy-start(bf16[512,2,64]{0,2,1:T(8,128)(2,1)} %pad_maximum_fusion.3) | copy-start | bytes 393220
  1483.3 13.7 copy-start.3
  1483.3 13.7 copy-start.4
  1483.3 13.7 copy-start.5
  1483.3 13.7 copy-start.6
  1483.3 13.7 copy-start.7
  1483.3 13.7 copy-start.8
  1497.0 22.7 %copy-start.1 = (f32[64,64]{0,1:T(8,128)S(1)}, f32[64,64]{0,1:T(8,128)}, u32[]{:S(2)}) copy-start(f32[64,64]{0,1:T(8,128)} %multiply_multiply_fusion.1) | copy-start | bytes 49156
  1497.0 22.7 %copy-start.2 = (f32[128,64]{0,1:T(8,128)S(1)}, f32[128,64]{0,1:T(8,128)}, u32[]{:S(2)}) copy-start(f32[128,64]{0,1:T(8,128)} %multiply_multiply_fusion.2) | copy-start | bytes 98308
  1497.0 42.6 %copy-start.10 = (f32[8]{0:T(128)S(1)}, f32[8]{0:T(128)}, u32[]{:S(2)}) copy-start(f32[8]{0:T(128)} %mul.534) | copy-start | bytes 100
where the time goes:
time: 1580 us; the launch traced here: 1570 us
  local copies, waits for them, and re-layouts  841 us (53%)
  blocking collectives  293 us (19%)
  waiting for transfers between devices  182 us (12%)
  other arithmetic  139 us (9%)
  matrix products  103 us (7%)
    unnamed x35, local copies, waits for them, and re-layouts  369 us
    all_to_all x1, blocking collectives, body(): lax.all_to_all(first, 'col', split_axis=4, concat_axis=3, tiled=True)  267 us
    all_to_all x1, waiting for transfers between devices, body(): lax.all_to_all(second, 'row', split_axis=4, concat_axis=1, tiled=True)  182 us
    all_to_all x2, local copies, waits for them, and re-layouts, body(): lax.all_to_all(second, 'row', split_axis=4, concat_axis=1, tiled=True)  99.1 us
    unnamed x5, other arithmetic  72.9 us
    convert_element_type x1, local copies, waits for them, and re-layouts, body(): first = jnp.einsum('cabpk,pkqz->caqbz', modes, table, preferred_element_t...  70.2 us
    convert_element_type x1, local copies, waits for them, and re-layouts, body(): second = jnp.einsum('caqbz,qbpy->cazpy', moved, table, preferred_element_...  69.9 us
    all_to_all x2, local copies, waits for them, and re-layouts, body(): lax.all_to_all(first, 'col', split_axis=4, concat_axis=3, tiled=True)  67.6 us
  transfers between devices with their start and end apart: 1, of which 1 were waited for; matrix products, arithmetic and copies ran while one was open for 0% of the time, Pallas kernels for 0%

commit v1 on v0

v1 whole, which is shorter than its diff:
```python
import functools
import math

import jax
import jax.numpy as jnp
from jax import lax
from jax.experimental import pallas as pl
from jax.experimental.pallas import tpu as pltpu
from jax.sharding import PartitionSpec as P

VMEM_LIMIT = 60 * 1024 * 1024


def padded(count):
    return -(-count // 16) * 16


def angles(waves, points):
    cells = jnp.arange(points, dtype=jnp.int32)
    product = jnp.mod(waves[:, None] * cells[None, :], points)
    return product.astype(jnp.float32) * (2.0 * math.pi / points)


def z_table(modes, points, blocks):
    angle = angles(jnp.arange(modes, dtype=jnp.int32) - modes // 2, points)
    cosine = jnp.cos(angle).reshape(modes, blocks, 1, -1)
    sine = jnp.sin(angle).reshape(modes, blocks, 1, -1)
    table = jnp.concatenate(
        [jnp.concatenate([cosine, sine], 2), jnp.concatenate([-sine, cosine], 2)], 0
    )
    return table.reshape(2 * modes, 2 * points).astype(jnp.bfloat16)


def y_table(modes, points, sources, blocks):
    angle = angles(jnp.arange(modes, dtype=jnp.int32) - modes // 2, points).T
    both = jnp.stack([jnp.cos(angle), jnp.sin(angle)], 0)
    both = both.reshape(2, blocks, points // blocks, sources, modes // sources)
    extra = padded(modes // sources) - modes // sources
    both = jnp.pad(both, ((0, 0), (0, 0), (0, 0), (0, 0), (0, extra)))
    both = jnp.transpose(both, (1, 0, 2, 3, 4))
    return both.reshape(blocks, 2 * (points // blocks), -1).astype(jnp.bfloat16)


def x_table(count, points, sources):
    waves = jnp.arange(count, dtype=jnp.int32)
    angle = angles(waves, points)
    cosine = jnp.cos(angle).astype(jnp.bfloat16)
    sine = jnp.sin(angle).astype(jnp.bfloat16)
    factor = jnp.where(waves == 0, 1.0, 2.0).astype(jnp.bfloat16)[:, None]
    table = jnp.stack([factor * cosine, -(factor * sine)], 0)
    table = table.reshape(2, sources, count // sources, points)
    extra = padded(count // sources) - count // sources
    table = jnp.pad(table, ((0, 0), (0, 0), (0, extra), (0, 0)))
    return table.reshape(2, -1, points)


def estimate(rows, depth, columns):
    return pl.CostEstimate(
        flops=2 * rows * depth * columns,
        bytes_accessed=2 * (rows * depth + depth * columns + rows * columns),
        transcendentals=0,
    )


def along_z(modes_ref, table_ref, out_ref):
    slabs, ky = modes_ref.shape[1], modes_ref.shape[2]
    blocks, width = out_ref.shape[0], out_ref.shape[4]

    @pl.loop(0, slabs)
    def _(a):
        value = jnp.dot(modes_ref[0, a], table_ref[...], preferred_element_type=jnp.float32)
        value = value.astype(jnp.bfloat16)
        for block in range(blocks):
            out_ref[block, 0, a] = jnp.zeros(out_ref.shape[3:], jnp.bfloat16)
            out_ref[block, 0, a, 0:ky, :] = value[:, block * width : (block + 1) * width]


def along_y(moved_ref, table_ref, out_ref, total):
    slabs, width = moved_ref.shape[2], moved_ref.shape[4]
    half = width // 2
    rows = out_ref.shape[2]
    total[...] = jnp.zeros_like(total)
    group = 2 if slabs % 2 == 0 and width % 128 == 0 else 1
    for a in range(0, slabs, group):
        parts = [moved_ref[:, 0, a + g].reshape(-1, width) for g in range(group)]
        data = parts[0] if group == 1 else jnp.concatenate(parts, 1)
        product = jnp.dot(table_ref[0], data, preferred_element_type=jnp.float32)
        for g in range(group):
            by_cos = product[:rows, g * width : (g + 1) * width]
            by_sin = product[rows:, g * width : (g + 1) * width]
            turned = jnp.concatenate([-by_sin[:, half:], by_sin[:, :half]], 1)
            total[:, a + g, :] = by_cos + turned
    out_ref[0, 0] = total[...].astype(jnp.bfloat16)


def along_x(arrived_0, arrived_1, arrived_2, table_ref, phase_ref, weight_ref, cos_ref, sin_ref,
            velocity_ref, by_cos_ref, by_sin_ref, real_scr, imag_scr):
    ys, width = arrived_0.shape[2], arrived_0.shape[4]
    half = width // 2
    fields = []
    for c, arrived_ref in enumerate((arrived_0, arrived_1, arrived_2)):
        for y in range(ys):
            data = arrived_ref[:, 0, y].reshape(-1, width).T
            real_scr[c, y * half : (y + 1) * half, :] = data[:half]
            imag_scr[c, y * half : (y + 1) * half, :] = data[half:]
        field = jnp.dot(real_scr[c], table_ref[0], preferred_element_type=jnp.float32)
        field = field + jnp.dot(imag_scr[c], table_ref[1], preferred_element_type=jnp.float32)
        velocity_ref[c] = field.astype(jnp.bfloat16).reshape(velocity_ref.shape[1:])
        fields.append(field)
    f0, f1, f2 = fields
    trace = (f0 * f0 + f1 * f1 + f2 * f2) / 3.0
    stress = [f0 * f0 - trace, f1 * f1 - trace, f2 * f2 - trace, f0 * f1, f0 * f2, f1 * f2]
    mixed = None
    for index, part in enumerate(stress):
        line = jnp.dot(
            part.astype(jnp.bfloat16), phase_ref[...], preferred_element_type=jnp.float32
        )
        term = weight_ref[index : index + 1, :] * line
        mixed = term if mixed is None else mixed + term
    mixed = mixed.reshape(ys, half, -1)
    by_cos_ref[...] = jnp.sum(mixed * cos_ref[...][None], 1)
    by_sin_ref[...] = jnp.sum(mixed * sin_ref[...][None], 1)


def body(rows, cols, velocity_modes, wavenumbers, polar, azimuth):
    kx_local, ky_local, modes = velocity_modes.shape[1:]
    modes = modes // 2
    kx = kx_local * rows
    points = velocity_points(modes)
    y_local, z_local = points // rows, points // cols
    width = 2 * z_local
    ky_pad, kx_pad = padded(ky_local), padded(kx_local)

    table_z = z_table(modes, points, cols)
    table_y = y_table(modes, points, cols, rows)
    steps = 2 if kx_local % 2 == 0 else 1
    slabs = kx_local // steps
    arrived = []
    for c in range(3):
        first = pl.pallas_call(
            along_z,
            grid=(steps,),
            in_specs=[
                pl.BlockSpec((1, slabs, ky_local, 2 * modes), lambda i, c=c: (c, i, 0, 0)),
                pl.BlockSpec((2 * modes, 2 * points), lambda i: (0, 0)),
            ],
            out_specs=pl.BlockSpec((cols, 1, slabs, ky_pad, width), lambda i: (0, 0, i, 0, 0)),
            out_shape=jax.ShapeDtypeStruct((cols, 1, kx_local, ky_pad, width), jnp.bfloat16),
            compiler_params=pltpu.CompilerParams(vmem_limit_bytes=VMEM_LIMIT),
            cost_estimate=estimate(kx_local * ky_pad, 2 * modes, 2 * points),
            name=f"along_z_{c}",
        )(velocity_modes, table_z)
        moved = lax.all_to_all(first, "col", split_axis=0, concat_axis=0, tiled=True)
        second = pl.pallas_call(
            along_y,
            grid=(rows,),
            in_specs=[
                pl.BlockSpec((cols, 1, kx_local, ky_pad, width), lambda t: (0, 0, 0, 0, 0)),
                pl.BlockSpec((1, 2 * y_local, cols * ky_pad), lambda t: (t, 0, 0)),
            ],
            out_specs=pl.BlockSpec((1, 1, y_local, kx_pad, width), lambda t: (t, 0, 0, 0, 0)),
            out_shape=jax.ShapeDtypeStruct((rows, 1, y_local, kx_pad, width), jnp.bfloat16),
            scratch_shapes=[pltpu.VMEM((y_local, kx_pad, width), jnp.float32)],
            compiler_params=pltpu.CompilerParams(vmem_limit_bytes=VMEM_LIMIT),
            cost_estimate=estimate(2 * points, cols * ky_pad, kx_local * width),
            name=f"along_y_{c}",
        )(moved, table_y)
        arrived.append(lax.all_to_all(second, "row", split_axis=0, concat_axis=0, tiled=True))

    dirs, freqs = polar.shape[0], wavenumbers.shape[0]
    count = dirs * freqs
    wave_j = jnp.repeat(wavenumbers, dirs)
    axis_one = jnp.tile(jnp.sin(polar) * jnp.cos(azimuth), freqs)
    axis_two = jnp.tile(jnp.sin(polar) * jnp.sin(azimuth), freqs)
    axis_three = jnp.tile(jnp.cos(polar), freqs)
    unit = 2.0 * math.pi / points
    x_pos = jnp.arange(points, dtype=jnp.int32).astype(jnp.float32) * unit
    angle_x = wave_j[None, :] * (axis_one[None, :] * x_pos[:, None])
    phase_x = jnp.concatenate([jnp.cos(angle_x), -jnp.sin(angle_x)], 1).astype(jnp.bfloat16)
    weights = jnp.stack(
        [
            axis_one * axis_one,
            axis_two * axis_two,
            axis_three * axis_three,
            2.0 * axis_one * axis_two,
            2.0 * axis_one * axis_three,
            2.0 * axis_two * axis_three,
        ],
        0,
    )
    weights = jnp.concatenate([weights, weights], 1)
    z_index = lax.axis_index("col") * z_local + jnp.arange(z_local, dtype=jnp.int32)
    y_index = lax.axis_index("row") * y_local + jnp.arange(y_local, dtype=jnp.int32)
    angle_z = wave_j[None, :] * (axis_three[None, :] * (z_index.astype(jnp.float32) * unit)[:, None])
    angle_y = wave_j[None, :] * (axis_two[None, :] * (y_index.astype(jnp.float32) * unit)[:, None])
    cos_z, sin_z = jnp.cos(angle_z), jnp.sin(angle_z)

    ys = 8
    whole = lambda i: (0, 0)
    velocity, by_cos, by_sin = pl.pallas_call(
        along_x,
        grid=(y_local // ys,),
        in_specs=[
            *[pl.BlockSpec((rows, 1, ys, kx_pad, width), lambda i: (0, 0, i, 0, 0))] * 3,
            pl.BlockSpec((2, rows * kx_pad, points), lambda i: (0, 0, 0)),
            pl.BlockSpec((points, 2 * count), whole),
            pl.BlockSpec((6, 2 * count), whole),
            pl.BlockSpec((z_local, 2 * count), whole),
            pl.BlockSpec((z_local, 2 * count), whole),
        ],
        out_specs=[
            pl.BlockSpec((3, ys, z_local, points), lambda i: (0, i, 0, 0)),
            pl.BlockSpec((ys, 2 * count), lambda i: (i, 0)),
            pl.BlockSpec((ys, 2 * count), lambda i: (i, 0)),
        ],
        out_shape=[
            jax.ShapeDtypeStruct((3, y_local, z_local, points), jnp.bfloat16),
            jax.ShapeDtypeStruct((y_local, 2 * count), jnp.float32),
            jax.ShapeDtypeStruct((y_local, 2 * count), jnp.float32),
        ],
        scratch_shapes=[pltpu.VMEM((3, ys * z_local, rows * kx_pad), jnp.bfloat16)] * 2,
        compiler_params=pltpu.CompilerParams(vmem_limit_bytes=VMEM_LIMIT),
        name="along_x",
    )(
        *arrived,
        x_table(kx, points, rows),
        phase_x,
        weights,
        jnp.concatenate([cos_z, cos_z], 1),
        jnp.concatenate([sin_z, sin_z], 1),
    )
    real_part = by_cos[:, :count] + by_sin[:, count:]
    imag_part = by_cos[:, count:] - by_sin[:, :count]
    cos_y, sin_y = jnp.cos(angle_y), jnp.sin(angle_y)
    terms = jnp.stack(
        [
            jnp.sum(real_part * cos_y + imag_part * sin_y, 0),
            jnp.sum(imag_part * cos_y - real_part * sin_y, 0),
        ],
        0,
    )
    spectrum = terms.reshape(2, freqs, dirs) * (wavenumbers * wavenumbers)[None, :, None]
    spectrum = jnp.transpose(spectrum / points**1.5, (2, 0, 1))
    total = lax.psum(spectrum, ("row", "col"))
    owned = dirs // cols
    far_field = lax.dynamic_slice_in_dim(total, lax.axis_index("col") * owned, owned, 0)
    return (velocity, far_field)


def velocity_points(modes):
    return 1 << (modes - 1).bit_length()


def solution(mesh):
    return jax.shard_map(
        functools.partial(body, mesh.shape["row"], mesh.shape["col"]),
        mesh=mesh,
        in_specs=(P(None, "row", "col", None), P(), P(), P()),
        out_specs=(P(None, "row", "col", None), P("col", None, None)),
        check_vma=False,
    )
```

time: 1580 us -> 638 us (0.40)
  local copies, waits for them, and re-layouts: 841 us -> 5.7 us
  blocking collectives: 293 us -> 37.6 us
  waiting for transfers between devices: 182 us -> 402 us
  Pallas kernels: 0 us -> 144 us
  other arithmetic: 139 us -> 15.1 us
  matrix products: 103 us -> 0 us
  starting transfers between devices: 7.49 us -> 32.4 us
    unnamed x35 -> x7, local copies, waits for them, and re-layouts: 369 us -> 0.66 us
    all_to_all x1 -> x0, blocking collectives: 267 us -> none  [body(): lax.all_to_all(first, 'col', split_axis=4, concat_axis=3, tiled=True)]
    all_to_all x1 -> x6, waiting for transfers between devices: 182 us -> 402 us  [the longest x3 227 us: body(): lax.all_to_all(first, 'col', split_axis=0, concat_axis=0, tiled=True)]
    all_to_all x4 -> x0, local copies, waits for them, and re-layouts: 167 us -> none  [the longest x2 99.1 us: body(): lax.all_to_all(second, 'row', split_axis=4, concat_axis=1, tiled=True)]
    pallas_call x0 -> x7, Pallas kernels: none -> 144 us  [the longest x3 58.8 us: body(): pl.pallas_call(along_z, grid=(steps,), in_specs=[pl.BlockSpec((1, slabs,...]
    convert_element_type x2 -> x4, local copies, waits for them, and re-layouts: 140 us -> 4.03 us  [the longest x3 2.48 us: y_table(): return both.reshape(blocks, 2 * (points // blocks), -1).astype(jnp.bfloat16)]
    dot_general x4 -> x0, matrix products: 103 us -> none  [the longest x1 33.4 us: body(): jnp.einsum('cazpy,pax->cyzx', arrived, table_x, preferred_element_type=jn...]
    unnamed x5 -> x0, other arithmetic: 72.9 us -> none
  transfers between devices with their start and end apart: 1 -> 6, of which waited for: 1 -> 6; matrix products, arithmetic and copies ran while one was open for 0% -> 2% of each run, Pallas kernels for 0% -> 13%
where the time goes in v1:
time: 638 us
  waiting for transfers between devices  402 us (63%)
  Pallas kernels  144 us (23%)
  blocking collectives  37.6 us (6%)
  starting transfers between devices  32.4 us (5%)
  other arithmetic  15.1 us (2%)
    all_to_all x3, waiting for transfers between devices, body(): lax.all_to_all(first, 'col', split_axis=0, concat_axis=0, tiled=True)  227 us
    all_to_all x3, waiting for transfers between devices, body(): lax.all_to_all(second, 'row', split_axis=0, concat_axis=0, tiled=True)  175 us
    pallas_call x3, Pallas kernels, body(): pl.pallas_call(along_z, grid=(steps,), in_specs=[pl.BlockSpec((1, slabs,...  58.8 us
    pallas_call x3, Pallas kernels, body(): pl.pallas_call(along_y, grid=(rows,), in_specs=[pl.BlockSpec((cols, 1, kx...  44.4 us
    pallas_call x1, Pallas kernels, body(): pl.pallas_call(along_x, grid=(y_local // ys,), in_specs=[*[pl.BlockSpec((...  40.9 us
    psum x1, blocking collectives, body(): total = lax.psum(spectrum, ('row', 'col'))  37.6 us
    all_to_all x3, starting transfers between devices, body(): lax.all_to_all(first, 'col', split_axis=0, concat_axis=0, tiled=True)  16.4 us
    all_to_all x3, starting transfers between devices, body(): lax.all_to_all(second, 'row', split_axis=0, concat_axis=0, tiled=True)  15.9 us
  transfers between devices with their start and end apart: 6, of which 6 were waited for; matrix products, arithmetic and copies ran while one was open for 2% of the time, Pallas kernels for 13%

profile of v1, /device:TPU:0, one launch (start us, length us, event | category | flops | bytes accessed | tf_op | source)
XLA Modules:
  0.0 637.7 jit_solution(4326331050244163407)
XLA Ops:
  0.7 3.6 fusion.19
  4.2 0.6 maximum_maximum_fusion
  4.9 1.6 copy.14.table_ref
  6.4 19.6 %along_z_2.1 = bf16[8,1,44,48,128]{4,3,2,1,0:T(8,128)(2,1)} custom-call(bf16[3,44,44,704]{3,2,1,0:T(8,128)(2,1)} %modes_ref.5, bf16[704,1024]{1,0:T(8,128)(2,1)} %copy.14.table_ref), custom_call_target="tpu_custom_call" | custom-call | flops 3045064704 | bytes 8740864 | tf_op jit(solution)/shard_map/along_z_2/pallas_call | solution.py:140
  26.0 7.3 %all-to-all-start.4 = ((bf16[8,1,44,48,128]{4,3,2,1,0:T(8,128)(2,1)}), bf16[8,1,44,48,128]{4,3,2,1,0:T(8,128)(2,1)}, u32[]{:S(2)}, u32[]{:S(2)}) async-start(bf16[8,1,44,48,128]{4,3,2,1,0:T(8,128)(2,1)} %along_z_2.1), calls=%async_computation.4 | async-start | bytes 8650752 | tf_op jit(solution)/shard_map/all_to_all | solution.py:153
  33.3 19.6 %along_z_1.1 = bf16[8,1,44,48,128]{4,3,2,1,0:T(8,128)(2,1)} custom-call(bf16[3,44,44,704]{3,2,1,0:T(8,128)(2,1)} %modes_ref.5, bf16[704,1024]{1,0:T(8,128)(2,1)} %copy.14.table_ref), custom_call_target="tpu_custom_call" | custom-call | flops 3045064704 | bytes 8740864 | tf_op jit(solution)/shard_map/along_z_1/pallas_call | solution.py:140
  52.9 76.5 %all-to-all-done.4.moved_ref = bf16[8,1,44,48,128]{4,3,2,1,0:T(8,128)(2,1)} async-done(((bf16[8,1,44,48,128]{4,3,2,1,0:T(8,128)(2,1)}), bf16[8,1,44,48,128]{4,3,2,1,0:T(8,128)(2,1)}, u32[]{:S(2)}, u32[]{:S(2)}) %all-to-all-start.4) | async-done | bytes 4325408 | tf_op jit(solution)/shard_map/all_to_all | solution.py:153
  129.4 4.6 all-to-all-start.2
  134.0 19.6 %along_z_0.1 = bf16[8,1,44,48,128]{4,3,2,1,0:T(8,128)(2,1)} custom-call(bf16[3,44,44,704]{3,2,1,0:T(8,128)(2,1)} %modes_ref.5, bf16[704,1024]{1,0:T(8,128)(2,1)} %copy.14.table_ref), custom_call_target="tpu_custom_call" | custom-call | flops 3045064704 | bytes 8740864 | tf_op jit(solution)/shard_map/along_z_0/pallas_call | solution.py:140
  153.6 75.7 %all-to-all-done.2.moved_ref = bf16[8,1,44,48,128]{4,3,2,1,0:T(8,128)(2,1)} async-done(((bf16[8,1,44,48,128]{4,3,2,1,0:T(8,128)(2,1)}), bf16[8,1,44,48,128]{4,3,2,1,0:T(8,128)(2,1)}, u32[]{:S(2)}, u32[]{:S(2)}) %all-to-all-start.2) | async-done | bytes 4325408 | tf_op jit(solution)/shard_map/all_to_all | solution.py:153
  229.3 4.6 all-to-all-start
  233.9 3.2 cosine_convert_fusion.1
  237.2 0.8 copy.15
  238.1 0.5 convert_element_type.132
  238.6 1.2 copy.16.table_ref
  239.7 14.8 %along_y_2.1 = bf16[4,1,128,48,128]{4,3,2,1,0:T(8,128)(2,1)} custom-call(bf16[8,1,44,48,128]{4,3,2,1,0:T(8,128)(2,1)} %all-to-all-done.4.moved_ref, bf16[4,256,384]{2,1,0:T(8,128)(2,1)} %copy.16.table_ref), custom_call_target="tpu_custom_call" | custom-call | flops 4429185024 | bytes 16646144 | tf_op jit(solution)/shard_map/along_y_2/pallas_call | solution.py:154
  254.5 74.7 %all-to-all-done.moved_ref = bf16[8,1,44,48,128]{4,3,2,1,0:T(8,128)(2,1)} async-done(((bf16[8,1,44,48,128]{4,3,2,1,0:T(8,128)(2,1)}), bf16[8,1,44,48,128]{4,3,2,1,0:T(8,128)(2,1)}, u32[]{:S(2)}, u32[]{:S(2)}) %all-to-all-start) | async-done | bytes 4325408 | tf_op jit(solution)/shard_map/all_to_all | solution.py:153
  329.2 5.3 all-to-all-start.5
  334.5 14.8 %along_y_1.1 = bf16[4,1,128,48,128]{4,3,2,1,0:T(8,128)(2,1)} custom-call(bf16[8,1,44,48,128]{4,3,2,1,0:T(8,128)(2,1)} %all-to-all-done.2.moved_ref, bf16[4,256,384]{2,1,0:T(8,128)(2,1)} %copy.16.table_ref), custom_call_target="tpu_custom_call" | custom-call | flops 4429185024 | bytes 16646144 | tf_op jit(solution)/shard_map/along_y_1/pallas_call | solution.py:154
  349.3 55.8 %all-to-all-done.5.arrived_2 = bf16[4,1,128,48,128]{4,3,2,1,0:T(8,128)(2,1)} async-done(((bf16[4,1,128,48,128]{4,3,2,1,0:T(8,128)(2,1)}), bf16[4,1,128,48,128]{4,3,2,1,0:T(8,128)(2,1)}, u32[]{:S(2)}, u32[]{:S(2)}) %all-to-all-start.5) | async-done | bytes 6291488 | tf_op jit(solution)/shard_map/all_to_all | solution.py:168
  405.2 5.4 all-to-all-start.3
  410.6 14.8 %along_y_0.1 = bf16[4,1,128,48,128]{4,3,2,1,0:T(8,128)(2,1)} custom-call(bf16[8,1,44,48,128]{4,3,2,1,0:T(8,128)(2,1)} %all-to-all-done.moved_ref, bf16[4,256,384]{2,1,0:T(8,128)(2,1)} %copy.16.table_ref), custom_call_target="tpu_custom_call" | custom-call | flops 4429185024 | bytes 16646144 | tf_op jit(solution)/shard_map/along_y_0/pallas_call | solution.py:154
  425.4 55.7 %all-to-all-done.3.arrived_1 = bf16[4,1,128,48,128]{4,3,2,1,0:T(8,128)(2,1)} async-done(((bf16[4,1,128,48,128]{4,3,2,1,0:T(8,128)(2,1)}), bf16[4,1,128,48,128]{4,3,2,1,0:T(8,128)(2,1)}, u32[]{:S(2)}, u32[]{:S(2)}) %all-to-all-start.3) | async-done | bytes 6291488 | tf_op jit(solution)/shard_map/all_to_all | solution.py:168
  481.1 5.3 all-to-all-start.1
  486.4 0.1 mul.512
  486.5 0.1 tile.34
  486.6 0.1 mul.521
  486.7 0.1 tile.32
  486.8 0.1 mul.493
  486.9 0.1 mul.501
  487.0 0.1 mul.506
  487.2 0.1 mul.490
  487.3 0.7 pad_maximum_fusion.3.weight_ref
  488.0 0.2 fusion.26
  488.2 0.7 pad_maximum_fusion.1
  488.9 1.1 cosine_convert_fusion.3
  490.1 0.8 pad_maximum_fusion.phase_ref
  490.8 1.9 fusion.21
  492.7 0.8 fusion.15
  493.5 63.5 %all-to-all-done.1.arrived_0 = bf16[4,1,128,48,128]{4,3,2,1,0:T(8,128)(2,1)} async-done(((bf16[4,1,128,48,128]{4,3,2,1,0:T(8,128)(2,1)}), bf16[4,1,128,48,128]{4,3,2,1,0:T(8,128)(2,1)}, u32[]{:S(2)}, u32[]{:S(2)}) %all-to-all-start.1) | async-done | bytes 6291488 | tf_op jit(solution)/shard_map/all_to_all | solution.py:168
  557.0 40.9 %along_x.1 = (bf16[3,128,64,512]{3,2,1,0:T(8,128)(2,1)}, f32[128,128]{1,0:T(8,128)}, f32[128,128]{1,0:T(8,128)}) custom-call(bf16[4,1,128,48,128]{4,3,2,1,0:T(8,128)(2,1)} %all-to-all-done.1.arrived_0, bf16[4,1,128,48,128]{4,3,2,1,0:T(8,128)(2,1)} %all-to-all-done.3.arrived_1, bf16[4,1,128,48,128]{4,3,2,1,0:T(8,128)(2,1)} %all-to-all-done.5.arrived_2, ...), custom_call_target="tpu_custom_call" | custom-call | tf_op jit(solution)/shard_map/along_x/pallas_call | solution.py:200
  597.9 1.3 add_reduce_fusion
  599.2 0.1 stack.15
  599.3 0.1 stack.32
  599.4 0.1 fusion.29
  599.4 37.6 %psum.7 = f32[8,2,8]{0,2,1:T(8,128)S(1)} all-reduce(f32[8,2,8]{0,2,1:T(8,128)S(1)} %fusion.29), channel_id=1, replica_groups=mesh['row'=4,'col'=8] {'row','col'}, use_global_device_ids=true, to_apply=%region_2.3 | all-reduce | flops 128 | bytes 1024 | tf_op jit(solution)/shard_map/psum | solution.py:244
  637.0 0.1 constant_dynamic-slice_fusion
  637.1 0.6 copy.22
  (28 shorter events, 0.3 us)
Async XLA Ops:
  26.0 103.4 %all-to-all-start.4 = ((bf16[8,1,44,48,128]{4,3,2,1,0:T(8,128)(2,1)}), bf16[8,1,44,48,128]{4,3,2,1,0:T(8,128)(2,1)}, u32[]{:S(2)}, u32[]{:S(2)}) async-start(bf16[8,1,44,48,128]{4,3,2,1,0:T(8,128)(2,1)} %along_z_2.1), calls=%async_computation.4 | async-start | bytes 8650752 | tf_op jit(solution)/shard_map/all_to_all | solution.py:153
  129.4 99.9 %all-to-all-start.2 = ((bf16[8,1,44,48,128]{4,3,2,1,0:T(8,128)(2,1)}), bf16[8,1,44,48,128]{4,3,2,1,0:T(8,128)(2,1)}, u32[]{:S(2)}, u32[]{:S(2)}) async-start(bf16[8,1,44,48,128]{4,3,2,1,0:T(8,128)(2,1)} %along_z_1.1), calls=%async_computation.2 | async-start | bytes 8650752 | tf_op jit(solution)/shard_map/all_to_all | solution.py:153
  229.3 99.9 %all-to-all-start = ((bf16[8,1,44,48,128]{4,3,2,1,0:T(8,128)(2,1)}), bf16[8,1,44,48,128]{4,3,2,1,0:T(8,128)(2,1)}, u32[]{:S(2)}, u32[]{:S(2)}) async-start(bf16[8,1,44,48,128]{4,3,2,1,0:T(8,128)(2,1)} %along_z_0.1), calls=%async_computation | async-start | bytes 8650752 | tf_op jit(solution)/shard_map/all_to_all | solution.py:153
  329.2 75.9 %all-to-all-start.5 = ((bf16[4,1,128,48,128]{4,3,2,1,0:T(8,128)(2,1)}), bf16[4,1,128,48,128]{4,3,2,1,0:T(8,128)(2,1)}, u32[]{:S(2)}, u32[]{:S(2)}) async-start(bf16[4,1,128,48,128]{4,3,2,1,0:T(8,128)(2,1)} %along_y_2.1), calls=%async_computation.5 | async-start | bytes 12582912 | tf_op jit(solution)/shard_map/all_to_all | solution.py:168
  405.2 75.9 %all-to-all-start.3 = ((bf16[4,1,128,48,128]{4,3,2,1,0:T(8,128)(2,1)}), bf16[4,1,128,48,128]{4,3,2,1,0:T(8,128)(2,1)}, u32[]{:S(2)}, u32[]{:S(2)}) async-start(bf16[4,1,128,48,128]{4,3,2,1,0:T(8,128)(2,1)} %along_y_1.1), calls=%async_computation.3 | async-start | bytes 12582912 | tf_op jit(solution)/shard_map/all_to_all | solution.py:168
  425.4 61.0 %copy-start.2 = (f32[8]{0:T(128)S(1)}, f32[8]{0:T(128)}, u32[]{:S(2)}) copy-start(f32[8]{0:T(128)} %param.6) | copy-start | bytes 100
  425.4 61.2 %copy-start = (f32[8]{0:T(128)S(1)}, f32[8]{0:T(128)}, u32[]{:S(2)}) copy-start(f32[8]{0:T(128)} %param.7) | copy-start | bytes 100
  425.4 61.4 %copy-start.1 = (f32[8]{0:T(128)S(1)}, f32[8]{0:T(128)}, u32[]{:S(2)}) copy-start(f32[8]{0:T(128)} %param.5) | copy-start | bytes 100
  481.1 75.9 %all-to-all-start.1 = ((bf16[4,1,128,48,128]{4,3,2,1,0:T(8,128)(2,1)}), bf16[4,1,128,48,128]{4,3,2,1,0:T(8,128)(2,1)}, u32[]{:S(2)}, u32[]{:S(2)}) async-start(bf16[4,1,128,48,128]{4,3,2,1,0:T(8,128)(2,1)} %along_y_0.1), calls=%async_computation.1 | async-start | bytes 12582912 | tf_op jit(solution)/shard_map/all_to_all | solution.py:168
